TPU v7x, 128 devices: a whole 4x4x4 slice. The times are simulated.
128 devices in a mesh: wide: 8 (over x, y_hi), narrow: 16 (over y_lo, z, core).
Axes of the slice: x: 4, y: 4 (y_hi: 2, y_lo: 2; y = y_hi * 2 + y_lo), z: 4, core: 2. Of those that a mesh axis runs over, the one named last changes fastest.
Arguments:
- mixture: bfloat16 [4, 256, 256, 256], P(None, ('wide', 'narrow')), may hold values from -30 to 30
- w_attn: bfloat16 [2, 4, 256, 256], replicated, may hold values from -2.625 to 2.625
- w_up: bfloat16 [2, 256, 1024], replicated, may hold values from -0.375 to 0.375
- w_down: bfloat16 [2, 1024, 256], replicated, may hold values from -0.1875 to 0.1875
- norm_gain: float32 [2, 2, 256], replicated, may hold values from 0.1 to 1.9
- norm_bias: float32 [2, 2, 256], replicated, may hold values from -3 to 3
- group_gain: float32 [2, 256], replicated, may hold values from 0.1 to 1.9
- group_bias: float32 [2, 256], replicated, may hold values from -3 to 3
Outputs:
- separated: bfloat16 [4, 256, 256, 256], P(None, ('wide', 'narrow'))
All inputs are finite; a program needn't handle non-finite values.
Results may differ from a plain program's by a relative error of at most 0.0083.
Values may be sent and summed in bfloat16 or wider, within the bound.
A program may use at most 64 MiB of HBM per device.

v0:
```python
import math

import jax
import jax.numpy as jnp
from jax import lax
from jax.sharding import Mesh
from jax.sharding import PartitionSpec as P

HEADS = 8
WIDE_NARROW = ("wide_0", "wide_1", "narrow_0", "narrow_1", "narrow_2")


EPSILON = 1e-05


def one_axis_at_a_time(value, axes):
    for axis in axes:
        value = lax.psum(value, axis)
    return value


def grouped_exchange(value, axis, split_dim, concat_dim, work, item_dim, out_dim):

    def moved(group):
        return lax.all_to_all(group, axis, split_axis=split_dim, concat_axis=concat_dim, tiled=True)

    items = jax.tree.leaves(value)[0].shape[item_dim]
    ends = [items * k // 2 for k in range(2 + 1)] if items % 2 == 0 else [0, items]
    groups = [
        jax.tree.map(lambda a: lax.slice_in_dim(a, low, high, axis=item_dim), value)
        for low, high in zip(ends, ends[1:])
    ]
    arrived = [moved(group) for group in groups]
    made = [work(group) for group in arrived]
    return jax.tree.map(lambda *parts: jnp.concatenate(parts, axis=out_dim), *made)


def positions_table(seq_length, model_width):
    positions = jnp.arange(seq_length, dtype=jnp.float32)[:, None]
    freq_index = jnp.arange(model_width // 2, dtype=jnp.float32)[None, :]
    angles = positions * jnp.exp(freq_index * (-2.0 * math.log(10000.0) / model_width))
    return jnp.concatenate([jnp.sin(angles), jnp.cos(angles)], axis=1)


def layer_norm(values, gain_row, bias_row):
    mean_value = jnp.mean(values, axis=-1, keepdims=True)
    centered = values - mean_value
    variance = jnp.mean(centered * centered, axis=-1, keepdims=True)
    return centered * lax.rsqrt(variance + EPSILON) * gain_row + bias_row


def encoder_block(seq_block, pos_table, attn_weights, up_weight, down_weight, gains, biases):
    groups, seq_length, inner_count, model_width = seq_block.shape
    head_size = model_width // HEADS
    state_rows = seq_block.astype(jnp.float32) + pos_table[None, :, None, :]
    normed = (
        layer_norm(state_rows, gains[0], biases[0]).astype(jnp.bfloat16).reshape(-1, model_width)
    )

    def project(matrix):
        product = jnp.dot(normed, matrix, preferred_element_type=jnp.float32).astype(jnp.bfloat16)
        return product.reshape(groups, seq_length, inner_count, HEADS, head_size)

    queries = project(attn_weights[0])
    key_rows = project(attn_weights[1])
    value_rows = project(attn_weights[2])
    scores = jnp.einsum("alnhe,amnhe->anhlm", queries, key_rows, preferred_element_type=jnp.float32)
    scores = scores * (1.0 / math.sqrt(head_size))
    shifted = jnp.exp(scores - jnp.max(scores, axis=-1, keepdims=True))
    weights = (shifted / jnp.sum(shifted, axis=-1, keepdims=True)).astype(jnp.bfloat16)
    attended = jnp.einsum(
        "anhlm,amnhe->alnhe", weights, value_rows, preferred_element_type=jnp.float32
    )
    attended = attended.astype(jnp.bfloat16).reshape(-1, model_width)
    mixed = jnp.dot(attended, attn_weights[3], preferred_element_type=jnp.float32)
    state_after = state_rows + mixed.reshape(state_rows.shape)
    normed_two = (
        layer_norm(state_after, gains[1], biases[1]).astype(jnp.bfloat16).reshape(-1, model_width)
    )
    hidden = jax.nn.relu(jnp.dot(normed_two, up_weight, preferred_element_type=jnp.float32)).astype(
        jnp.bfloat16
    )
    output = jnp.dot(hidden, down_weight, preferred_element_type=jnp.float32)
    return state_after + output.reshape(state_after.shape)


def run_layer(seq_data, layer_index, w_attn, w_up, w_down, norm_gain, norm_bias, block_rows):
    seq_count, seq_length, inner_count, model_width = seq_data.shape
    per_block = math.gcd(seq_count, max(1, block_rows // (seq_length * inner_count)))
    pos_table = positions_table(seq_length, model_width)
    blocked = seq_data.reshape(
        seq_count // per_block, per_block, seq_length, inner_count, model_width
    )

    def apply_block(seq_block):
        return encoder_block(
            seq_block,
            pos_table,
            w_attn[layer_index],
            w_up[layer_index],
            w_down[layer_index],
            norm_gain[layer_index],
            norm_bias[layer_index],
        )

    return lax.map(apply_block, blocked).reshape(seq_count, seq_length, inner_count, model_width)


def group_norm(values, gain_row, bias_row):
    cell_count = values.shape[1] * lax.axis_size(WIDE_NARROW) * values.shape[2] * values.shape[3]
    totals, squares = (
        one_axis_at_a_time(jnp.sum(values, axis=(1, 2, 3)), WIDE_NARROW),
        one_axis_at_a_time(jnp.sum(values * values, axis=(1, 2, 3)), WIDE_NARROW),
    )
    mean_flat = totals / cell_count
    variance = squares / cell_count - mean_flat * mean_flat
    centered = values - mean_flat[:, None, None, None]
    return centered * lax.rsqrt(variance[:, None, None, None] + EPSILON) * gain_row + bias_row


def on_device(mixture, w_attn, w_up, w_down, norm_gain, norm_bias, group_gain, group_bias):
    mix_count, segs_here, frame_count, model_width = mixture.shape
    intra_out = run_layer(
        mixture.reshape(mix_count * segs_here, frame_count, 1, model_width),
        0,
        w_attn,
        w_up,
        w_down,
        norm_gain,
        norm_bias,
        512,
    ).reshape(mixture.shape)
    carried = (
        group_norm(intra_out, group_gain[0], group_bias[0]) + mixture.astype(jnp.float32)
    ).astype(jnp.bfloat16)

    def inter_layer(regrouped):
        return run_layer(regrouped, 1, w_attn, w_up, w_down, norm_gain, norm_bias, 512).astype(
            jnp.bfloat16
        )

    def across(regrouped):
        result = inter_layer(regrouped)
        return lax.all_to_all(result, WIDE_NARROW, split_axis=1, concat_axis=2, tiled=True)

    inter_out = grouped_exchange(carried, WIDE_NARROW, 2, 1, across, 0, 0)
    separated = group_norm(
        inter_out.astype(jnp.float32), group_gain[1], group_bias[1]
    ) + carried.astype(jnp.float32)
    return separated.astype(jnp.bfloat16)


def solution(mesh):
    split = Mesh(
        mesh.devices.reshape(4, 2, 2, 4, 2),
        ("wide_0", "wide_1", "narrow_0", "narrow_1", "narrow_2"),
    )
    placed = (P(None, WIDE_NARROW, None, None), P(), P(), P(), P(), P(), P(), P())
    return jax.shard_map(
        on_device,
        mesh=split,
        in_specs=placed,
        out_specs=P(None, WIDE_NARROW, None, None),
        check_vma=False,
    )
```

profile of v0, /device:TPU:1, one launch (start us, length us, event | category | flops | bytes accessed | tf_op | source)
XLA Modules:
  0.0 284.9 jit_solution(17898310136358450638)
XLA Ops:
  0.6 69.5 %while.30 = (s32[]{:T(128)}, f32[4,2,256,1,256]{4,2,1,3,0:T(8,128)S(1)}, bf16[4,2,256,1,256]{4,2,1,3,0:T(8,128)(2,1)}, f32[256,256]{1,0:T(8,128)S(1)}, f32[2,2,2...) while((s32[]{:T(128)}, ...), condition=%wide.region_7.8_spmd, body=%wide.region_0.7_spmd.sunk | while | flops 950011136 | bytes 32064172 | solution.py:106
  7.5 3.5 %fusion.260 = (f32[2,8,256]{2,1,0:T(8,128)S(1)}, f32[2,8,256,256]{2,3,1,0:T(8,128)}) fusion(bf16[2,256,8,32]{1,0,3,2:T(2,128)(2,1)S(1)} %reshape.1409, bf16[2,256,8,32]{1,0,3,2:T(2,128)(2,1)S(1)} %reshape.1410), kind=kOutput, calls=%fused_computation.192.clone.1 | convolution fusion | flops 70254848 | bytes 4734976 | tf_op jit(solution)/shard_map/while/body/eval_jaxpr/sub | solution.py:69
  12.4 2.6 fusion.261
  15.0 1.5 fusion.262
  24.9 3.4 %fusion.260 = (f32[2,8,256]{2,1,0:T(8,128)S(1)}, f32[2,8,256,256]{2,3,1,0:T(8,128)}) fusion(bf16[2,256,8,32]{1,0,3,2:T(2,128)(2,1)S(1)} %reshape.1409, bf16[2,256,8,32]{1,0,3,2:T(2,128)(2,1)S(1)} %reshape.1410), kind=kOutput, calls=%fused_computation.192.clone.1 | convolution fusion | flops 70254848 | bytes 4734976 | tf_op jit(solution)/shard_map/while/body/eval_jaxpr/sub | solution.py:69
  29.7 2.6 fusion.261
  32.4 1.5 fusion.262
  42.3 3.4 %fusion.260 = (f32[2,8,256]{2,1,0:T(8,128)S(1)}, f32[2,8,256,256]{2,3,1,0:T(8,128)}) fusion(bf16[2,256,8,32]{1,0,3,2:T(2,128)(2,1)S(1)} %reshape.1409, bf16[2,256,8,32]{1,0,3,2:T(2,128)(2,1)S(1)} %reshape.1410), kind=kOutput, calls=%fused_computation.192.clone.1 | convolution fusion | flops 70254848 | bytes 4734976 | tf_op jit(solution)/shard_map/while/body/eval_jaxpr/sub | solution.py:69
  47.1 2.6 fusion.261
  49.7 1.5 fusion.262
  59.6 3.4 %fusion.260 = (f32[2,8,256]{2,1,0:T(8,128)S(1)}, f32[2,8,256,256]{2,3,1,0:T(8,128)}) fusion(bf16[2,256,8,32]{1,0,3,2:T(2,128)(2,1)S(1)} %reshape.1409, bf16[2,256,8,32]{1,0,3,2:T(2,128)(2,1)S(1)} %reshape.1410), kind=kOutput, calls=%fused_computation.192.clone.1 | convolution fusion | flops 70254848 | bytes 4734976 | tf_op jit(solution)/shard_map/while/body/eval_jaxpr/sub | solution.py:69
  64.4 2.6 fusion.261
  67.1 1.5 fusion.262
  71.8 9.3 %all-reduce.3 = (f32[4]{0:T(128)S(1)}, f32[4]{0:T(128)S(1)}) all-reduce(f32[4]{0:T(128)S(1)} %fusion.132, f32[4]{0:T(128)S(1)} %reduce_sum.171), channel_id=1, replica_groups=mesh['wide_0'=4,'wide_1'=2,'narrow_0'=2,'narrow_1'=4,'narrow_2'=2] {'wid..., use_global_device_ids=true, to_apply=%region_15.16 | all-reduce | flops 8 | bytes 64 | tf_op jit(solution)/shard_map/psum | solution.py:18
  81.1 5.3 %all-reduce.9 = (f32[4]{0:T(128)S(1)}, f32[4]{0:T(128)S(1)}) all-reduce(f32[4]{0:T(128)S(1)} %get-tuple-element.211, f32[4]{0:T(128)S(1)} %get-tuple-element.212), channel_id=1, replica_groups=mesh['wide_0'=4,'wide_1'=2,'narrow_0'=2,'narrow_1'=4,'narrow_2'=2] {'wid..., use_global_device_ids=true, to_apply=%region_16.17 | all-reduce | flops 8 | bytes 64 | tf_op jit(solution)/shard_map/psum | solution.py:18
  86.4 3.8 %all-reduce.7 = (f32[4]{0:T(128)S(1)}, f32[4]{0:T(128)S(1)}) all-reduce(f32[4]{0:T(128)S(1)} %get-tuple-element.223, f32[4]{0:T(128)S(1)} %get-tuple-element.224), channel_id=1, replica_groups=mesh['wide_0'=4,'wide_1'=2,'narrow_0'=2,'narrow_1'=4,'narrow_2'=2] {'nar..., use_global_device_ids=true, to_apply=%region_17.18 | all-reduce | flops 8 | bytes 64 | tf_op jit(solution)/shard_map/psum | solution.py:18
  90.1 9.7 %all-reduce.1 = (f32[4]{0:T(128)S(1)}, f32[4]{0:T(128)S(1)}) all-reduce(f32[4]{0:T(128)S(1)} %get-tuple-element.219, f32[4]{0:T(128)S(1)} %get-tuple-element.220), channel_id=1, replica_groups=mesh['wide_0'=4,'wide_1'=2,'narrow_0'=2,'narrow_1'=4,'narrow_2'=2] {'nar..., use_global_device_ids=true, to_apply=%region_18.19 | all-reduce | flops 8 | bytes 64 | tf_op jit(solution)/shard_map/psum | solution.py:18
  99.8 9.1 %all-reduce.5 = (f32[4]{0:T(128)S(1)}, f32[4]{0:T(128)S(1)}) all-reduce(f32[4]{0:T(128)S(1)} %get-tuple-element.207, f32[4]{0:T(128)S(1)} %get-tuple-element.208), channel_id=1, replica_groups=mesh['wide_0'=4,'wide_1'=2,'narrow_0'=2,'narrow_1'=4,'narrow_2'=2] {'nar..., use_global_device_ids=true, to_apply=%region_19.20 | all-reduce | flops 8 | bytes 64 | tf_op jit(solution)/shard_map/psum | solution.py:18
  111.9 5.0 %all-to-all-start = ((bf16[2,2,256,256]{3,1,0,2:T(2,128)(2,1)}), bf16[2,2,256,256]{3,1,0,2:T(2,128)(2,1)S(1)}, u32[]{:S(2)}, u32[]{:S(2)}) async-start(bf16[2,2,256,256]{3,1,0,2:T(2,128)(2,1)} %copy.149), calls=%async_computation | async-start | bytes 1048576 | tf_op jit(solution)/shard_map/all_to_all | solution.py:25
  118.2 12.2 %all-to-all-done = bf16[2,2,256,256]{3,1,0,2:T(2,128)(2,1)S(1)} async-done(((bf16[2,2,256,256]{3,1,0,2:T(2,128)(2,1)}), bf16[2,2,256,256]{3,1,0,2:T(2,128)(2,1)S(1)}, u32[]{:S(2)}, u32[]{:S(2)}) %all-to-all-start) | async-done | bytes 524320 | tf_op jit(solution)/shard_map/all_to_all | solution.py:25
  130.4 5.7 %all-to-all-start.2 = ((bf16[2,2,256,256]{3,1,0,2:T(2,128)(2,1)}), bf16[2,2,256,256]{3,1,0,2:T(2,128)(2,1)}, u32[]{:S(2)}, u32[]{:S(2)}) async-start(bf16[2,2,256,256]{3,1,0,2:T(2,128)(2,1)} %copy.153), calls=%async_computation.2 | async-start | bytes 1048576 | tf_op jit(solution)/shard_map/all_to_all | solution.py:25
  137.8 38.2 %while.31 = (s32[]{:T(128)}, bf16[2,1,256,2,256]{4,3,0,2,1:T(2,128)(2,1)}, bf16[2,1,256,2,256]{4,2,3,1,0:T(8,128)(2,1)S(1)}, f32[256,256]{1,0:T(8,128)S(1)}, f32...) while((s32[]{:T(128)}, ...), condition=%wide.region_27.28_spmd, body=%wide.region_20.27_spmd.sunk | while | flops 951190784 | bytes 39142060 | solution.py:106
  142.7 3.0 %fusion.283 = (f32[2,8,256]{2,1,0:T(8,128)S(1)}, f32[2,8,256,256]{2,3,1,0:T(8,128)}) fusion(f32[2,8,256,256]{2,3,1,0:T(8,128)S(1)} %fusion.282), kind=kOutput, calls=%fused_computation.196.clone.1 | output fusion | flops 4194559 | bytes 8404992 | tf_op jit(solution)/shard_map/while/body/eval_jaxpr/sub | solution.py:69
  147.3 2.8 fusion.284
  152.2 1.5 maximum_convert_fusion.7
  154.2 1.6 fusion.286
  161.8 3.0 %fusion.283 = (f32[2,8,256]{2,1,0:T(8,128)S(1)}, f32[2,8,256,256]{2,3,1,0:T(8,128)}) fusion(f32[2,8,256,256]{2,3,1,0:T(8,128)S(1)} %fusion.282), kind=kOutput, calls=%fused_computation.196.clone.1 | output fusion | flops 4194559 | bytes 8404992 | tf_op jit(solution)/shard_map/while/body/eval_jaxpr/sub | solution.py:69
  166.4 2.8 fusion.284
  171.3 1.5 maximum_convert_fusion.7
  173.3 1.6 fusion.286
  176.0 10.4 %all-to-all-start.1 = ((bf16[2,256,2,256]{3,2,0,1:T(2,128)(2,1)}), bf16[2,256,2,256]{3,2,0,1:T(2,128)(2,1)}, u32[]{:S(2)}, u32[]{:S(2)}) async-start(bf16[2,256,2,256]{3,2,0,1:T(2,128)(2,1)} %bitcast.396), calls=%async_computation.1 | async-start | bytes 1048576 | tf_op jit(solution)/shard_map/all_to_all | solution.py:144
  189.1 38.3 %while.32 = (s32[]{:T(128)}, bf16[2,1,256,2,256]{4,3,0,2,1:T(2,128)(2,1)}, bf16[2,1,256,2,256]{4,2,3,1,0:T(8,128)(2,1)S(1)}, f32[256,256]{1,0:T(8,128)S(1)}, f32...) while((s32[]{:T(128)}, ...), condition=%wide.region_35.36_spmd, body=%wide.region_28.35_spmd.sunk | while | flops 951190784 | bytes 39142060 | solution.py:106
  194.1 3.0 %fusion.306 = (f32[2,8,256]{2,1,0:T(8,128)S(1)}, f32[2,8,256,256]{2,3,1,0:T(8,128)}) fusion(f32[2,8,256,256]{2,3,1,0:T(8,128)S(1)} %fusion.305), kind=kOutput, calls=%fused_computation.200.clone.1 | output fusion | flops 4194559 | bytes 8404992 | tf_op jit(solution)/shard_map/while/body/eval_jaxpr/sub | solution.py:69
  198.6 2.8 fusion.307
  203.5 1.5 maximum_convert_fusion.8
  205.5 1.6 fusion.309
  213.2 3.0 %fusion.306 = (f32[2,8,256]{2,1,0:T(8,128)S(1)}, f32[2,8,256,256]{2,3,1,0:T(8,128)}) fusion(f32[2,8,256,256]{2,3,1,0:T(8,128)S(1)} %fusion.305), kind=kOutput, calls=%fused_computation.200.clone.1 | output fusion | flops 4194559 | bytes 8404992 | tf_op jit(solution)/shard_map/while/body/eval_jaxpr/sub | solution.py:69
  217.8 2.8 fusion.307
  222.7 1.5 maximum_convert_fusion.8
  224.6 1.6 fusion.309
  227.4 9.8 %all-to-all-start.3 = ((bf16[2,256,2,256]{3,2,0,1:T(2,128)(2,1)}), bf16[2,256,2,256]{3,2,0,1:T(2,128)(2,1)S(1)}, u32[]{:S(2)}, u32[]{:S(2)}) async-start(bf16[2,256,2,256]{3,2,0,1:T(2,128)(2,1)} %bitcast.395), calls=%async_computation.3 | async-start | bytes 1048576 | tf_op jit(solution)/shard_map/all_to_all | solution.py:144
  238.8 11.9 %all-to-all-done.3 = bf16[2,256,2,256]{3,2,0,1:T(2,128)(2,1)S(1)} async-done(((bf16[2,256,2,256]{3,2,0,1:T(2,128)(2,1)}), bf16[2,256,2,256]{3,2,0,1:T(2,128)(2,1)S(1)}, u32[]{:S(2)}, u32[]{:S(2)}) %all-to-all-start.3) | async-done | bytes 524320 | tf_op jit(solution)/shard_map/all_to_all | solution.py:144
  251.7 7.0 %all-reduce.2 = (f32[4]{0:T(128)S(1)}, f32[4]{0:T(128)S(1)}) all-reduce(f32[4]{0:T(128)S(1)} %get-tuple-element.150, f32[4]{0:T(128)S(1)} %get-tuple-element.149), channel_id=1, replica_groups=mesh['wide_0'=4,'wide_1'=2,'narrow_0'=2,'narrow_1'=4,'narrow_2'=2] {'wid..., use_global_device_ids=true, to_apply=%region_43.44 | all-reduce | flops 8 | bytes 64 | tf_op jit(solution)/shard_map/psum | solution.py:18
  258.7 5.3 %all-reduce.8 = (f32[4]{0:T(128)S(1)}, f32[4]{0:T(128)S(1)}) all-reduce(f32[4]{0:T(128)S(1)} %get-tuple-element.209, f32[4]{0:T(128)S(1)} %get-tuple-element.210), channel_id=1, replica_groups=mesh['wide_0'=4,'wide_1'=2,'narrow_0'=2,'narrow_1'=4,'narrow_2'=2] {'wid..., use_global_device_ids=true, to_apply=%region_44.45 | all-reduce | flops 8 | bytes 64 | tf_op jit(solution)/shard_map/psum | solution.py:18
  264.0 3.9 %all-reduce.6 = (f32[4]{0:T(128)S(1)}, f32[4]{0:T(128)S(1)}) all-reduce(f32[4]{0:T(128)S(1)} %get-tuple-element.221, f32[4]{0:T(128)S(1)} %get-tuple-element.222), channel_id=1, replica_groups=mesh['wide_0'=4,'wide_1'=2,'narrow_0'=2,'narrow_1'=4,'narrow_2'=2] {'nar..., use_global_device_ids=true, to_apply=%region_45.46 | all-reduce | flops 8 | bytes 64 | tf_op jit(solution)/shard_map/psum | solution.py:18
  267.9 6.6 %all-reduce = (f32[4]{0:T(128)S(1)}, f32[4]{0:T(128)S(1)}) all-reduce(f32[4]{0:T(128)S(1)} %get-tuple-element.217, f32[4]{0:T(128)S(1)} %get-tuple-element.218), channel_id=1, replica_groups=mesh['wide_0'=4,'wide_1'=2,'narrow_0'=2,'narrow_1'=4,'narrow_2'=2] {'nar..., use_global_device_ids=true, to_apply=%region_46.47 | all-reduce | flops 8 | bytes 64 | tf_op jit(solution)/shard_map/psum | solution.py:18
  274.5 8.9 %all-reduce.4 = (f32[4]{0:T(128)S(1)}, f32[4]{0:T(128)S(1)}) all-reduce(f32[4]{0:T(128)S(1)} %get-tuple-element.205, f32[4]{0:T(128)S(1)} %get-tuple-element.206), channel_id=1, replica_groups=mesh['wide_0'=4,'wide_1'=2,'narrow_0'=2,'narrow_1'=4,'narrow_2'=2] {'nar..., use_global_device_ids=true, to_apply=%region_47.48 | all-reduce | flops 8 | bytes 64 | tf_op jit(solution)/shard_map/psum | solution.py:18
  283.4 1.5 fusion.125
  (257 shorter events, 92.6 us)
Async XLA Ops:
  15.0 2.1 copy-start.14
  15.0 2.5 copy-start.3
  32.3 2.1 copy-start.14
  32.3 2.5 copy-start.3
  49.7 2.1 copy-start.14
  49.7 2.5 copy-start.3
  67.1 2.1 copy-start.14
  67.1 2.5 copy-start.3
  70.0 0.7 copy-start.12
  70.0 1.2 copy-start.13
  70.1 38.9 %copy-start = (bf16[4,2,256,1,256]{4,2,1,3,0:T(8,128)(2,1)S(1)}, bf16[4,2,256,1,256]{4,2,1,3,0:T(8,128)(2,1)}, u32[]{:S(2)}) copy-start(bf16[4,2,256,1,256]{4,2,1,3,0:T(8,128)(2,1)} %get-tuple-element.574) | copy-start | bytes 3145732
  109.5 1.0 copy-start.1
  111.9 18.5 %all-to-all-start = ((bf16[2,2,256,256]{3,1,0,2:T(2,128)(2,1)}), bf16[2,2,256,256]{3,1,0,2:T(2,128)(2,1)S(1)}, u32[]{:S(2)}, u32[]{:S(2)}) async-start(bf16[2,2,256,256]{3,1,0,2:T(2,128)(2,1)} %copy.149), calls=%async_computation | async-start | bytes 1048576 | tf_op jit(solution)/shard_map/all_to_all | solution.py:25
  118.2 19.6 %copy-start.8 = (f32[2,2,256]{2,1,0:T(2,128)S(1)}, f32[2,2,256]{2,1,0:T(2,128)}, u32[]{:S(2)}) copy-start(f32[2,2,256]{2,1,0:T(2,128)} %get-tuple-element.583) | copy-start | bytes 12292
  118.2 19.6 %copy-start.9 = (f32[2,2,256]{2,1,0:T(2,128)S(1)}, f32[2,2,256]{2,1,0:T(2,128)}, u32[]{:S(2)}) copy-start(f32[2,2,256]{2,1,0:T(2,128)} %get-tuple-element.585) | copy-start | bytes 12292
  130.4 45.6 %all-to-all-start.2 = ((bf16[2,2,256,256]{3,1,0,2:T(2,128)(2,1)}), bf16[2,2,256,256]{3,1,0,2:T(2,128)(2,1)}, u32[]{:S(2)}, u32[]{:S(2)}) async-start(bf16[2,2,256,256]{3,1,0,2:T(2,128)(2,1)} %copy.153), calls=%async_computation.2 | async-start | bytes 1048576 | tf_op jit(solution)/shard_map/all_to_all | solution.py:25
  154.1 1.6 copy-start.6
  156.1 0.8 copy-start.7
  173.3 1.6 copy-start.6
  175.2 0.8 copy-start.7
  176.0 51.4 %all-to-all-start.1 = ((bf16[2,256,2,256]{3,2,0,1:T(2,128)(2,1)}), bf16[2,256,2,256]{3,2,0,1:T(2,128)(2,1)}, u32[]{:S(2)}, u32[]{:S(2)}) async-start(bf16[2,256,2,256]{3,2,0,1:T(2,128)(2,1)} %bitcast.396), calls=%async_computation.1 | async-start | bytes 1048576 | tf_op jit(solution)/shard_map/all_to_all | solution.py:144
  205.5 1.6 copy-start.4
  207.4 0.8 copy-start.5
  224.6 1.6 copy-start.4
  226.6 0.8 copy-start.5
  227.4 23.3 %all-to-all-start.3 = ((bf16[2,256,2,256]{3,2,0,1:T(2,128)(2,1)}), bf16[2,256,2,256]{3,2,0,1:T(2,128)(2,1)S(1)}, u32[]{:S(2)}, u32[]{:S(2)}) async-start(bf16[2,256,2,256]{3,2,0,1:T(2,128)(2,1)} %bitcast.395), calls=%async_computation.3 | async-start | bytes 1048576 | tf_op jit(solution)/shard_map/all_to_all | solution.py:144
  238.6 44.8 %copy-start.2 = (bf16[4,2,256,256]{3,2,1,0:T(8,128)(2,1)S(1)}, bf16[4,2,256,256]{3,2,1,0:T(8,128)(2,1)}, u32[]{:S(2)}) copy-start(bf16[4,2,256,256]{3,2,1,0:T(8,128)(2,1)} %copy-done.1) | copy-start | bytes 3145732
  238.6 44.8 %copy-start.10 = (f32[1,256]{1,0:T(1,128)S(1)}, f32[1,256]{1,0:T(1,128)}, u32[]{:S(2)}) copy-start(f32[1,256]{1,0:T(1,128)} %get-tuple-element.257) | copy-start | bytes 3076
  238.6 44.8 %copy-start.11 = (f32[1,256]{1,0:T(1,128)S(1)}, f32[1,256]{1,0:T(1,128)}, u32[]{:S(2)}) copy-start(f32[1,256]{1,0:T(1,128)} %get-tuple-element.259) | copy-start | bytes 3076
where the time goes:
time: 287 us; the launch traced here: 285 us
  matrix products  92.1 us (32%)
  blocking collectives  68.7 us (24%)
  other arithmetic  35.9 us (13%)
  local copies, waits for them, and re-layouts  31.7 us (11%)
  starting transfers between devices  30.8 us (11%)
  waiting for transfers between devices  24.1 us (8%)
    psum x10, blocking collectives, one_axis_at_a_time(): value = lax.psum(value, axis)  68.7 us
    dot_general x24, matrix products, project(): jnp.dot(normed, matrix, preferred_element_type=jnp.float32)  27 us
    dot_general x8, matrix products, encoder_block(): jnp.einsum('anhlm,amnhe->alnhe', weights, value_rows, preferred_element_t...  21.5 us
    all_to_all x2, starting transfers between devices, across(): lax.all_to_all(result, WIDE_NARROW, split_axis=1, concat_axis=2, tiled=True)  20.1 us
    sub x4, matrix products, encoder_block(): shifted = jnp.exp(scores - jnp.max(scores, axis=-1, keepdims=True))  13.8 us
    all_to_all x2, waiting for transfers between devices, moved(): lax.all_to_all(group, axis, split_axis=split_dim, concat_axis=concat_dim,...  12.2 us
    sub x4, other arithmetic, encoder_block(): shifted = jnp.exp(scores - jnp.max(scores, axis=-1, keepdims=True))  12 us
    all_to_all x2, waiting for transfers between devices, across(): lax.all_to_all(result, WIDE_NARROW, split_axis=1, concat_axis=2, tiled=True)  11.9 us
  transfers between devices with their start and end apart: 4, of which 2 were waited for; matrix products, arithmetic and copies ran while one was open for 28% of the time, Pallas kernels for 0%

commit v1 on v0

v1 whole, which is shorter than its diff:
```python
import math

import jax
import jax.numpy as jnp
import numpy as np
from jax import lax
from jax.experimental import pallas as pl
from jax.experimental.pallas import tpu as pltpu
from jax.sharding import PartitionSpec as P

F32 = jnp.float32
BF = jnp.bfloat16
MESH = pl.DeviceIdType.MESH

HEADS = 8
HEAD = 32
D = 256
LENGTH = 256
MIX = 4
PLANE = 16
COLUMN = 8
EPSILON = 1e-05
QUERY_SCALE = math.log2(math.e) / math.sqrt(HEAD)
SEQ_CELLS = float(LENGTH * D)
UNIT_CELLS = 2.0 * SEQ_CELLS
COLUMN_CELLS = UNIT_CELLS * COLUMN
MIX_CELLS = COLUMN_CELLS * PLANE


def position_tables():
    positions = np.arange(LENGTH, dtype=np.float32)[:, None]
    freq = np.arange(D // 2, dtype=np.float32)[None, :]
    angles = positions * np.exp(freq * np.float32(-2.0 * math.log(10000.0) / D))
    table = np.concatenate([np.sin(angles), np.cos(angles)], axis=1).astype(np.float32)
    r, p, s = np.meshgrid(np.arange(COLUMN), np.arange(PLANE), np.arange(2), indexing="ij")
    order = (16 * p + 2 * r + s).reshape(-1)
    return np.stack([table, table[order]])


def dot(a, b):
    return jnp.dot(a, b, preferred_element_type=F32)


def layer_norm(rows, gain, bias):
    mean = jnp.mean(rows, axis=-1, keepdims=True)
    centered = rows - mean
    variance = jnp.mean(centered * centered, axis=-1, keepdims=True)
    return centered * lax.rsqrt(variance + EPSILON) * gain + bias


def encoder(state, gains, biases, qv_t, wk, wo, up, down):
    normed = layer_norm(state, gains[0:1], biases[0:1]).astype(BF)
    both = lax.dot_general(qv_t, normed, (((1,), (1,)), ((), ())), preferred_element_type=F32)
    queries = (both[:D] * QUERY_SCALE).astype(BF)
    values = both[D:].astype(BF)
    keys = dot(normed, wk).astype(BF)
    ones = jnp.ones((16, LENGTH), BF)
    heads = []
    for h in range(HEADS):
        rows = slice(h * HEAD, (h + 1) * HEAD)
        scores = dot(keys[:, rows], queries[rows])
        top = jnp.max(scores, axis=0, keepdims=True)
        weights = jnp.exp2(scores - top).astype(BF)
        summed = dot(jnp.concatenate([values[rows], ones], axis=0), weights)
        heads.append((summed[:HEAD] * (1.0 / summed[HEAD : HEAD + 1])).astype(BF))
    attended = jnp.concatenate(heads, axis=0).T
    after = state + dot(attended, wo)
    normed = layer_norm(after, gains[1:2], biases[1:2]).astype(BF)
    out = after
    for c in range(4):
        hidden = slice(c * 256, (c + 1) * 256)
        active = jnp.maximum(dot(normed, up[:, hidden]), 0.0).astype(BF)
        out = out + dot(active, down[hidden])
    return out


def combine(total, spread, count, cells):
    whole = jnp.sum(total, axis=0, keepdims=True)
    offset = total - whole * (1.0 / count)
    square = jnp.sum(spread, axis=0, keepdims=True)
    return whole, square + jnp.sum(offset * offset, axis=0, keepdims=True) * (1.0 / cells)


def pack_stats(total, spread):
    row = lax.broadcasted_iota(jnp.int32, (8, 128), 0)
    wide_total = jnp.broadcast_to(total, (8, 128))
    return jnp.where(row == 0, wide_total, jnp.broadcast_to(spread, (8, 128)))


def kernel(
    mix_ref, attn_ref, up_ref, down_ref, gain_ref, bias_ref, ggain_ref, gbias_ref, pos_ref,
    out_ref,
    state, qv_t, y, carried, plane_in, column_out, inter, column_in, plane_out, back, flat,
    half, stat_own, stat_a, stat_mid, stat_b, sent, recv, load_sem,
):
    index = lax.axis_index("wide") * 16 + lax.axis_index("narrow")
    plane = lax.div(index, 8)
    column = lax.rem(index, 8)

    def device(p, r):
        return (lax.div(p, 2), lax.rem(p, 2) * 8 + r)

    def each_column(work):
        def one(k, _):
            work(lax.rem(column + k, COLUMN))
            return 0

        lax.fori_loop(1, COLUMN, one, 0)

    def each_plane(work):
        def one(k, _):
            work(lax.rem(plane + k, PLANE))
            return 0

        lax.fori_loop(1, PLANE, one, 0)

    def remote(src, dst, kind, slot, p, r):
        return pltpu.make_async_remote_copy(
            src_ref=src, dst_ref=dst, send_sem=sent.at[kind, slot], recv_sem=recv.at[kind, slot],
            device_id=device(p, r), device_id_type=MESH,
        )

    def arrived(ref, kind, slot):
        pltpu.make_async_copy(ref, ref, recv.at[kind, slot]).wait()

    def left(ref, kind, slot):
        pltpu.make_async_copy(ref, ref, sent.at[kind, slot]).wait()

    load = pltpu.make_async_copy(mix_ref, state.at[0], load_sem)
    load.start()

    barrier = pltpu.get_barrier_semaphore()
    each_column(
        lambda r: pl.semaphore_signal(
            barrier, inc=1, device_id=device(plane, r), device_id_type=MESH
        )
    )
    each_plane(
        lambda p: pl.semaphore_signal(
            barrier, inc=1, device_id=device(p, column), device_id_type=MESH
        )
    )
    pl.semaphore_wait(barrier, COLUMN - 1 + PLANE - 1)

    for l in range(2):
        for i, j in ((0, 0), (1, 2)):
            qv_t[l, i * D : (i + 1) * D] = attn_ref[l, j].T

    load.wait()

    def compute(t):
        l = lax.div(t, 8)
        b = lax.div(lax.rem(t, 8), 2)
        s = lax.rem(t, 2)
        start = state[l, b, s].astype(F32) + pos_ref[l]
        out = encoder(
            start, gain_ref[l], bias_ref[l], qv_t[l], attn_ref[l, 1], attn_ref[l, 3],
            up_ref.at[l], down_ref.at[l],
        )
        y[b, s] = out

        @pl.when(l == 1)
        def _():
            rounded = out.astype(BF)
            inter[b, s] = rounded
            y[b, s] = rounded.astype(F32)
            each_column(
                lambda r: remote(
                    inter.at[b, s, pl.ds(pl.multiple_of(r * 32, 32), 32)],
                    column_in.at[b, 2 * column + s],
                    4, b, plane, r,
                ).start()
            )
            mine = pl.ds(pl.multiple_of(column * 32, 32), 32)
            column_in[b, 2 * column + s] = inter[b, s, mine]

        done = y[b, s]
        total = jnp.sum(jnp.sum(done, axis=0, keepdims=True), axis=1, keepdims=True)
        offset = done - total * (1.0 / SEQ_CELLS)
        spread = jnp.sum(jnp.sum(offset * offset, axis=0, keepdims=True), axis=1, keepdims=True)
        half[s] = pack_stats(total, spread)

    def start_stats(slot):
        total, spread = combine(half[:, 0, :], half[:, 1, :], 2, SEQ_CELLS)
        packed = pack_stats(total, spread)
        stat_own[slot] = packed
        stat_a[slot, column] = packed
        each_column(
            lambda r: remote(
                stat_own.at[slot], stat_a.at[slot, column], 0, slot, plane, r
            ).start()
        )

    def relay_stats(slot):
        arrived(stat_a.at[slot, pl.ds(0, COLUMN - 1)], 0, slot)
        total, spread = combine(stat_a[slot, :, 0, :], stat_a[slot, :, 1, :], COLUMN, UNIT_CELLS)
        packed = pack_stats(total, spread)
        stat_mid[slot] = packed
        stat_b[slot, plane] = packed
        each_plane(
            lambda p: remote(
                stat_mid.at[slot], stat_b.at[slot, plane], 1, slot, p, column
            ).start()
        )

    def mixture_stats(slot):
        arrived(stat_b.at[slot, pl.ds(0, PLANE - 1)], 1, slot)
        total, spread = combine(stat_b[slot, :, 0, :], stat_b[slot, :, 1, :], PLANE, COLUMN_CELLS)
        mean = total * (1.0 / MIX_CELLS)
        scale = lax.rsqrt(spread * (1.0 / MIX_CELLS) + EPSILON)
        return (
            jnp.concatenate([mean, mean], axis=1),
            jnp.concatenate([scale, scale], axis=1),
        )

    def carry(b):
        mean, scale = mixture_stats(b)
        for s in range(2):
            normed = (y[b, s] - mean) * scale * ggain_ref[0:1] + gbias_ref[0:1]
            carried[b, s] = (normed + state[0, b, s].astype(F32)).astype(BF)
        mine = pl.ds(pl.multiple_of(plane * 16, 16), 16)
        plane_in[b, plane] = carried[b, :, mine, :]
        each_plane(
            lambda p: remote(
                carried.at[b, :, pl.ds(pl.multiple_of(p * 16, 16), 16), :],
                plane_in.at[b, plane],
                2, b, p, column,
            ).start()
        )

    def regroup(b):
        arrived(plane_in.at[b, pl.ds(0, PLANE - 1)], 2, b)
        for c in range(2):
            lanes = slice(c * 128, (c + 1) * 128)
            flat[c] = plane_in[b, :, :, :, lanes].reshape(512, 128).astype(F32)
            for f in range(16):
                column_out[b, f, :, lanes] = flat[c, pl.ds(f, 32, stride=16), :].astype(BF)
        mine = pl.ds(pl.multiple_of(column * 32, 32), 32)
        state[1, b, :, mine, :] = column_out[b, pl.ds(2 * column, 2)]
        each_column(
            lambda r: remote(
                column_out.at[b, pl.ds(2 * r, 2)], state.at[1, b, :, mine, :], 3, b, plane, r
            ).start()
        )

    def regroup_back(b):
        arrived(column_in.at[b, pl.ds(0, 2 * (COLUMN - 1))], 4, b)
        for c in range(2):
            lanes = slice(c * 128, (c + 1) * 128)
            flat[c] = column_in[b, :, :, lanes].reshape(512, 128).astype(F32)
            for q in range(32):
                plane_out[b, q, :, lanes] = flat[c, pl.ds(q, 16, stride=32), :].astype(BF)
        mine = pl.ds(pl.multiple_of(plane * 16, 16), 16)
        back[b, :, mine, :] = plane_out[b, pl.ds(2 * plane, 2)]
        each_plane(
            lambda p: remote(
                plane_out.at[b, pl.ds(2 * p, 2)], back.at[b, :, mine, :], 5, b, p, column
            ).start()
        )

    def finish(b):
        mean, scale = mixture_stats(4 + b)
        arrived(back.at[b, :, pl.ds(0, 16 * (PLANE - 1)), :], 5, b)
        for s in range(2):
            normed = (back[b, s].astype(F32) - mean) * scale * ggain_ref[1:2] + gbias_ref[1:2]
            out_ref[b, s] = (normed + carried[b, s].astype(F32)).astype(BF)

    def step(t, _):
        def when(first, last, parity, work):
            due = (t >= first) & (t <= last) & (lax.rem(t, 2) == parity)
            pl.when(due)(lambda: work(lax.div(t - first, 2)))

        @pl.when((t >= 8) & (t < 16) & (lax.rem(t, 2) == 0))
        def _():
            b = lax.div(t - 8, 2)
            arrived(state.at[1, b, :, pl.ds(0, 32 * (COLUMN - 1)), :], 3, b)

        @pl.when(t < 16)
        def _():
            compute(t)

        when(1, 15, 1, start_stats)
        when(2, 16, 0, relay_stats)
        when(3, 9, 1, carry)
        when(5, 11, 1, regroup)
        when(11, 17, 1, regroup_back)
        when(13, 19, 1, finish)
        return 0

    lax.fori_loop(0, 20, step, 0)

    def drain(b, _):
        for slot in (b, 4 + b):
            left(stat_a.at[slot, pl.ds(0, COLUMN - 1)], 0, slot)
            left(stat_b.at[slot, pl.ds(0, PLANE - 1)], 1, slot)
        left(plane_in.at[b, pl.ds(0, PLANE - 1)], 2, b)
        left(state.at[1, b, :, pl.ds(0, 32 * (COLUMN - 1)), :], 3, b)
        left(column_in.at[b, pl.ds(0, 2 * (COLUMN - 1))], 4, b)
        left(back.at[b, :, pl.ds(0, 16 * (PLANE - 1)), :], 5, b)
        return 0

    lax.fori_loop(0, MIX, drain, 0)


def on_device(mixture, w_attn, w_up, w_down, norm_gain, norm_bias, group_gain, group_bias):
    vmem = pl.BlockSpec(memory_space=pltpu.VMEM)
    return pl.pallas_call(
        kernel,
        name="dual_path",
        out_shape=jax.ShapeDtypeStruct(mixture.shape, BF),
        in_specs=[pl.BlockSpec(memory_space=pl.ANY)] + [vmem] * 8,
        out_specs=vmem,
        scratch_shapes=[
            pltpu.VMEM((2, MIX, 2, LENGTH, D), BF),
            pltpu.VMEM((2, 2 * D, D), BF),
            pltpu.VMEM((MIX, 2, LENGTH, D), F32),
            pltpu.VMEM((MIX, 2, LENGTH, D), BF),
            pltpu.VMEM((MIX, PLANE, 2, 16, D), BF),
            pltpu.VMEM((MIX, 16, 32, D), BF),
            pltpu.VMEM((MIX, 2, LENGTH, D), BF),
            pltpu.VMEM((MIX, 16, 32, D), BF),
            pltpu.VMEM((MIX, 32, 16, D), BF),
            pltpu.VMEM((MIX, 2, LENGTH, D), BF),
            pltpu.VMEM((2, 512, 128), F32),
            pltpu.VMEM((2, 8, 128), F32),
            pltpu.VMEM((8, 8, 128), F32),
            pltpu.VMEM((8, COLUMN, 8, 128), F32),
            pltpu.VMEM((8, 8, 128), F32),
            pltpu.VMEM((8, PLANE, 8, 128), F32),
            pltpu.SemaphoreType.DMA((6, 8)),
            pltpu.SemaphoreType.DMA((6, 8)),
            pltpu.SemaphoreType.DMA,
        ],
        compiler_params=pltpu.CompilerParams(
            collective_id=0, has_side_effects=True, vmem_limit_bytes=48 * 1024 * 1024
        ),
    )(
        mixture, w_attn, w_up, w_down, norm_gain, norm_bias, group_gain, group_bias,
        jnp.asarray(position_tables()),
    )


def solution(mesh):
    split = P(None, ("wide", "narrow"), None, None)
    return jax.shard_map(
        on_device, mesh=mesh, in_specs=(split,) + (P(),) * 7, out_specs=split, check_vma=False
    )
```

time: 287 us -> 102 us (0.36)
  matrix products: 92.1 us -> 0 us
  Pallas kernels: 0 us -> 91.7 us
  blocking collectives: 68.7 us -> 0 us
  other arithmetic: 35.9 us -> 0 us
  starting transfers between devices: 30.8 us -> 0 us
  waiting for transfers between devices: 24.1 us -> 0 us
  local copies, waits for them, and re-layouts: 31.7 us -> 9.65 us
    pallas_call x0 -> x1, Pallas kernels: none -> 91.7 us  [on_device(): pl.pallas_call(kernel, name='dual_path', out_shape=jax.ShapeDtypeStruct(m...]
    dot_general x60 -> x0, matrix products: 78.3 us -> none  [the longest x24 27 us: project(): jnp.dot(normed, matrix, preferred_element_type=jnp.float32)]
    psum x10 -> x0, blocking collectives: 68.7 us -> none  [one_axis_at_a_time(): value = lax.psum(value, axis)]
    all_to_all x4 -> x0, starting transfers between devices: 30.8 us -> none  [the longest x2 20.1 us: across(): lax.all_to_all(result, WIDE_NARROW, split_axis=1, concat_axis=2, tiled=True)]
    all_to_all x4 -> x0, waiting for transfers between devices: 24.1 us -> none  [the longest x2 12.2 us: moved(): lax.all_to_all(group, axis, split_axis=split_dim, concat_axis=concat_dim,...]
    reduce_sum x27 -> x0, other arithmetic: 13.8 us -> none  [the longest x16 7.8 us: layer_norm(): variance = jnp.mean(centered * centered, axis=-1, keepdims=True)]
    sub x4 -> x0, matrix products: 13.8 us -> none  [encoder_block(): shifted = jnp.exp(scores - jnp.max(scores, axis=-1, keepdims=True))]
    sub x4 -> x0, other arithmetic: 12 us -> none  [encoder_block(): shifted = jnp.exp(scores - jnp.max(scores, axis=-1, keepdims=True))]
  transfers between devices with their start and end apart: 4 -> 0, of which waited for: 2 -> 0; matrix products, arithmetic and copies ran while one was open for 28% -> 0% of each run, Pallas kernels for 0% -> 0%
where the time goes in v1:
time: 102 us; the launch traced here: 101 us
  Pallas kernels  91.7 us (90%)
  local copies, waits for them, and re-layouts  9.65 us (9%)
    pallas_call x1, Pallas kernels, on_device(): pl.pallas_call(kernel, name='dual_path', out_shape=jax.ShapeDtypeStruct(m...  91.7 us
    unnamed x19, local copies, waits for them, and re-layouts  9.65 us

profile of v1, /device:TPU:1, one launch (start us, length us, event | category | flops | bytes accessed | tf_op | source)
XLA Modules:
  0.0 101.4 jit_solution(170932866771223261)
XLA Ops:
  0.0 0.0 copy-start
  0.0 1.2 %copy-done = bf16[4,2,256,256]{3,2,1,0:T(8,128)(2,1)S(1)} copy-done((bf16[4,2,256,256]{3,2,1,0:T(8,128)(2,1)S(1)}, bf16[4,2,256,256]{3,2,1,0:T(8,128)(2,1)}, u32[]{:S(2)}) %copy-start) | copy-done | bytes 1048600
  1.2 0.0 copy-start.1
  1.2 1.2 %copy-done.1 = bf16[2,4,256,256]{3,2,1,0:T(8,128)(2,1)S(1)} copy-done((bf16[2,4,256,256]{3,2,1,0:T(8,128)(2,1)S(1)}, bf16[2,4,256,256]{3,2,1,0:T(8,128)(2,1)}, u32[]{:S(2)}) %copy-start.1) | copy-done | bytes 1048600
  2.5 0.0 copy-start.2
  2.5 1.2 %copy-done.2 = bf16[2,256,1024]{2,1,0:T(8,128)(2,1)S(1)} copy-done((bf16[2,256,1024]{2,1,0:T(8,128)(2,1)S(1)}, bf16[2,256,1024]{2,1,0:T(8,128)(2,1)}, u32[]{:S(2)}) %copy-start.2) | copy-done | bytes 1048600
  3.7 0.0 copy-start.3
  3.7 1.2 %copy-done.3 = bf16[2,1024,256]{2,1,0:T(8,128)(2,1)S(1)} copy-done((bf16[2,1024,256]{2,1,0:T(8,128)(2,1)S(1)}, bf16[2,1024,256]{2,1,0:T(8,128)(2,1)}, u32[]{:S(2)}) %copy-start.3) | copy-done | bytes 1048600
  4.9 0.0 copy-start.4
  4.9 1.0 %copy-done.4 = f32[2,256,256]{2,1,0:T(8,128)S(1)} copy-done((f32[2,256,256]{2,1,0:T(8,128)S(1)}, f32[2,256,256]{2,1,0:T(8,128)}, u32[]{:S(2)}) %copy-start.4) | copy-done | bytes 524312
  5.9 0.0 copy-start.5
  5.9 0.7 copy-done.5
  6.6 0.0 copy-start.6
  6.6 0.7 copy-done.6
  7.3 0.0 copy-start.7
  7.3 0.7 copy-done.7
  8.0 0.0 copy-start.8
  8.0 0.7 copy-done.8
  8.7 91.7 %dual_path.1 = bf16[4,2,256,256]{3,2,1,0:T(8,128)(2,1)S(1)} custom-call(bf16[4,2,256,256]{3,2,1,0:T(8,128)(2,1)S(1)} %copy-done, bf16[2,4,256,256]{3,2,1,0:T(8,128)(2,1)S(1)} %copy-done.1, bf16[2,256,1024]{2,1,0:T(8,128)(2,1)S(1)} %copy-done.2, bf16[2,1024,256]{2,1,0:T(8,128)(2,1)S(1)} %copy-done.3, f32[2,2,256]{2,1,0:T(2,128)S(1)} %copy-done.5, ...), custom_call_target="tpu_custom_call" | custom-call | tf_op jit(solution)/shard_map/dual_path/pallas_call | solution.py:307
  100.4 1.0 copy.11
Async XLA Ops:
  0.0 1.2 %copy-start = (bf16[4,2,256,256]{3,2,1,0:T(8,128)(2,1)S(1)}, bf16[4,2,256,256]{3,2,1,0:T(8,128)(2,1)}, u32[]{:S(2)}) copy-start(bf16[4,2,256,256]{3,2,1,0:T(8,128)(2,1)} %mix_ref.1) | copy-start | bytes 3145732
  1.2 1.2 %copy-start.1 = (bf16[2,4,256,256]{3,2,1,0:T(8,128)(2,1)S(1)}, bf16[2,4,256,256]{3,2,1,0:T(8,128)(2,1)}, u32[]{:S(2)}) copy-start(bf16[2,4,256,256]{3,2,1,0:T(8,128)(2,1)} %attn_ref.1) | copy-start | bytes 3145732
  2.5 1.2 %copy-start.2 = (bf16[2,256,1024]{2,1,0:T(8,128)(2,1)S(1)}, bf16[2,256,1024]{2,1,0:T(8,128)(2,1)}, u32[]{:S(2)}) copy-start(bf16[2,256,1024]{2,1,0:T(8,128)(2,1)} %up_ref.1) | copy-start | bytes 3145732
  3.7 1.2 %copy-start.3 = (bf16[2,1024,256]{2,1,0:T(8,128)(2,1)S(1)}, bf16[2,1024,256]{2,1,0:T(8,128)(2,1)}, u32[]{:S(2)}) copy-start(bf16[2,1024,256]{2,1,0:T(8,128)(2,1)} %down_ref.1) | copy-start | bytes 3145732
  4.9 1.0 %copy-start.4 = (f32[2,256,256]{2,1,0:T(8,128)S(1)}, f32[2,256,256]{2,1,0:T(8,128)}, u32[]{:S(2)}) copy-start(f32[2,256,256]{2,1,0:T(8,128)} %constant.2.clone.pos_ref) | copy-start | bytes 1572868
  5.9 0.7 copy-start.5
  6.6 0.7 copy-start.6
  7.3 0.7 copy-start.7
  8.0 0.7 copy-start.8

commit v2 on v1

v2 whole, which is shorter than its diff:
```python
import math

import jax
import jax.numpy as jnp
import numpy as np
from jax import lax
from jax.experimental import pallas as pl
from jax.experimental.pallas import tpu as pltpu
from jax.sharding import PartitionSpec as P

F32 = jnp.float32
BF = jnp.bfloat16
MESH = pl.DeviceIdType.MESH

HEADS = 8
HEAD = 32
D = 256
LENGTH = 256
MIX = 4
PLANE = 16
COLUMN = 8
CHIPS = 64
EPSILON = 1e-05
QUERY_SCALE = math.log2(math.e) / math.sqrt(HEAD)
UNIT_CELLS = 2.0 * LENGTH * D
COLUMN_CELLS = UNIT_CELLS * COLUMN
MIX_CELLS = COLUMN_CELLS * PLANE
FAR_FIRST = sorted(
    range(1, CHIPS), key=lambda k: -sum((0, 1, 2, 1)[k // d % 4] for d in (1, 4, 16))
)
S2_AT = 3
V_AT = 14
N_AT = 7
R_AT = 8
RR_AT = 20
F_AT = 22


def position_tables():
    positions = np.arange(LENGTH, dtype=np.float32)[:, None]
    freq = np.arange(D // 2, dtype=np.float32)[None, :]
    angles = positions * np.exp(freq * np.float32(-2.0 * math.log(10000.0) / D))
    table = np.concatenate([np.sin(angles), np.cos(angles)], axis=1).astype(np.float32)
    s, chip = np.meshgrid(np.arange(4), np.arange(CHIPS), indexing="ij")
    order = (4 * chip + s).reshape(-1)
    return np.stack([table, table[order]])


def dot(a, b):
    return jnp.dot(a, b, preferred_element_type=F32)


def layer_norm(rows, gain, bias):
    mean = jnp.mean(rows, axis=-1, keepdims=True)
    centered = rows - mean
    variance = jnp.mean(centered * centered, axis=-1, keepdims=True)
    return centered * lax.rsqrt(variance + EPSILON) * gain + bias


def attention(states, gain, bias, qv_t, wk, wo):
    normed = [layer_norm(state, gain, bias).astype(BF) for state in states]
    both = [
        lax.dot_general(qv_t, rows, (((1,), (1,)), ((), ())), preferred_element_type=F32)
        for rows in normed
    ]
    queries = [(part[:D] * QUERY_SCALE).astype(BF) for part in both]
    values = [part[D:].astype(BF) for part in both]
    keys = [dot(rows, wk).astype(BF) for rows in normed]
    ones = jnp.ones((16, LENGTH), BF)
    after = []
    for state, query, key, value in zip(states, queries, keys, values):
        rows = [slice(h * HEAD, (h + 1) * HEAD) for h in range(HEADS)]
        scores = [dot(key[:, r], query[r]) for r in rows]
        weights = [
            jnp.exp2(part - jnp.max(part, axis=0, keepdims=True)).astype(BF) for part in scores
        ]
        summed = [
            dot(jnp.concatenate([value[r], ones], axis=0), part) for r, part in zip(rows, weights)
        ]
        heads = [(part[:HEAD] * (1.0 / part[HEAD : HEAD + 1])).astype(BF) for part in summed]
        after.append(jnp.concatenate(heads, axis=0).T)
    return [state + dot(rows, wo) for state, rows in zip(states, after)]


def feed_forward(afters, gain, bias, up, down):
    normed = [layer_norm(after, gain, bias).astype(BF) for after in afters]
    active = [jnp.maximum(dot(rows, up), 0.0).astype(BF) for rows in normed]
    return [after + dot(rows, down) for after, rows in zip(afters, active)]


def combine(total, spread, count, cells):
    whole = jnp.sum(total, axis=0, keepdims=True)
    offset = total - whole * (1.0 / count)
    square = jnp.sum(spread, axis=0, keepdims=True)
    return whole, square + jnp.sum(offset * offset, axis=0, keepdims=True) * (1.0 / cells)


def pack_stats(total, spread):
    row = lax.broadcasted_iota(jnp.int32, (8, 128), 0)
    wide_total = jnp.broadcast_to(total, (8, 128))
    return jnp.where(row == 0, wide_total, jnp.broadcast_to(spread, (8, 128)))


def kernel(
    mix_ref, attn_hbm, up_hbm, down_hbm, gain_hbm, bias_hbm, ggain_hbm, gbias_hbm, pos_hbm,
    out_ref,
    attn_ref, up_ref, down_ref, gain_ref, bias_ref, ggain_ref, gbias_ref, pos_ref,
    state, qv_t, middle, y, carried, pair_in, chip_out, chip_in, back_out, back_in, pair_out,
    back, flat, partial, stat_own, stat_a, stat_mid, stat_b, sent, recv, load_sem,
):
    index = lax.axis_index("wide") * 16 + lax.axis_index("narrow")
    plane = lax.div(index, 8)
    column = lax.rem(index, 8)
    chip = lax.div(index, 2)
    core = lax.rem(index, 2)
    partner = column + 1 - 2 * core
    half = pl.ds(pl.multiple_of(core * 128, 128), 128)
    other_half = pl.ds(pl.multiple_of(128 - core * 128, 128), 128)

    def device(p, r):
        return (lax.div(p, 2), lax.rem(p, 2) * 8 + r)

    def each_column(work):
        for k in range(1, COLUMN):
            work(lax.rem(column + k, COLUMN))

    def each_plane(work):
        for k in range(1, PLANE):
            work(lax.rem(plane + k, PLANE))

    def each_chip(work):
        for k in FAR_FIRST:
            x = lax.rem(lax.div(chip, 16) + k // 16, 4)
            y_ = lax.rem(lax.div(lax.rem(chip, 16), 4) + k // 4 % 4, 4)
            z = lax.rem(lax.rem(chip, 4) + k % 4, 4)
            work(x, y_, z)

    def chip_device(x, y_, z, c):
        return (x * 2 + lax.div(y_, 2), lax.rem(y_, 2) * 8 + z * 2 + c)

    def remote(src, dst, kind, slot, where):
        return pltpu.make_async_remote_copy(
            src_ref=src, dst_ref=dst, send_sem=sent.at[kind, slot], recv_sem=recv.at[kind, slot],
            device_id=where, device_id_type=MESH,
        )

    def arrived(ref, kind, slot):
        pltpu.make_async_copy(ref, ref, recv.at[kind, slot]).wait()

    def left(ref, kind, slot):
        pltpu.make_async_copy(ref, ref, sent.at[kind, slot]).wait()

    loads = (
        ((mix_ref.at[0], state.at[0]), (attn_hbm.at[0], attn_ref.at[0]),
         (gain_hbm, gain_ref), (bias_hbm, bias_ref), (pos_hbm.at[0], pos_ref.at[0])),
        ((up_hbm.at[0], up_ref.at[0]), (down_hbm.at[0], down_ref.at[0])),
        ((mix_ref.at[pl.ds(1, MIX - 1)], state.at[pl.ds(1, MIX - 1)]),
         (ggain_hbm, ggain_ref), (gbias_hbm, gbias_ref)),
        ((attn_hbm.at[1], attn_ref.at[1]), (pos_hbm.at[1], pos_ref.at[1]),
         (up_hbm.at[1], up_ref.at[1]), (down_hbm.at[1], down_ref.at[1])),
    )
    loads = [
        [pltpu.make_async_copy(src, dst, load_sem.at[i, j]) for j, (src, dst) in enumerate(group)]
        for i, group in enumerate(loads)
    ]
    for group in loads:
        for copy in group:
            copy.start()

    def loaded(i):
        for copy in loads[i]:
            copy.wait()

    barrier = pltpu.get_barrier_semaphore()

    def greet(where):
        pl.semaphore_signal(barrier, inc=1, device_id=where, device_id_type=MESH)

    each_chip(lambda x, y_, z: greet(chip_device(x, y_, z, core)))
    for z in range(4):
        greet(device(plane, z * 2 + (1 - core)))

    def turn(l):
        for i, j in ((0, 0), (1, 2)):
            qv_t[l, i * D : (i + 1) * D] = attn_ref[l, j].T

    def first_half(t):
        l = lax.div(t, 8)
        b = lax.div(lax.rem(t, 8), 2)

        @pl.when(l == 0)
        def _():
            for s in range(2):
                middle[s] = state[b, s].astype(F32)

        @pl.when(l == 1)
        def _():
            arrived(chip_in.at[b, pl.ds(0, CHIPS - 1)], 3, b)
            for c in range(2):
                lanes = slice(c * 128, (c + 1) * 128)
                flat[c] = chip_in[b, :, :, lanes].reshape(512, 128).astype(F32)
                for f in range(2):
                    for s in range(4):
                        middle[f, s * CHIPS : (s + 1) * CHIPS, lanes] = flat[
                            c, pl.ds(4 * f + s, CHIPS, stride=8), :
                        ]

        starts = [middle[s] + pos_ref[l] for s in range(2)]
        after = attention(
            starts, gain_ref[l, 0:1], bias_ref[l, 0:1], qv_t[l], attn_ref[l, 1], attn_ref[l, 3]
        )
        for s in range(2):
            middle[s] = after[s]

    def second_half(t):
        l = lax.div(t, 8)
        b = lax.div(lax.rem(t, 8), 2)
        afters = [middle[s] for s in range(2)]
        outs = feed_forward(
            afters, gain_ref[l, 1:2], bias_ref[l, 1:2], up_ref[l], down_ref[l]
        )
        pivot = None
        for s in range(2):
            out = jnp.where(l == 0, outs[s], outs[s].astype(BF).astype(F32))
            y[b, s] = out
            if pivot is None:
                pivot = out[:8]
                near = square = jnp.zeros((8, D), F32)
            offset = out.reshape(LENGTH // 8, 8, D) - pivot[None]
            near = near + jnp.sum(offset, axis=0)
            square = square + jnp.sum(offset * offset, axis=0)
        partial[0] = pivot
        partial[1] = near
        partial[2] = square

    def send_back(b):
        for c in range(2):
            lanes = slice(c * 128, (c + 1) * 128)
            for f in range(2):
                for s in range(4):
                    flat[c, pl.ds(4 * f + s, CHIPS, stride=8), :] = y[
                        b, f, s * CHIPS : (s + 1) * CHIPS, lanes
                    ]
            back_out[b, :, :, lanes] = flat[c].reshape(CHIPS, 8, 128).astype(BF)
        back_in[b, chip] = back_out[b, chip]
        each_chip(
            lambda x, y_, z: remote(
                back_out.at[b, x * 16 + y_ * 4 + z], back_in.at[b, chip],
                4, b, chip_device(x, y_, z, core),
            ).start()
        )

    def start_stats(slot):
        near = partial[1]
        totals = near + partial[0] * 64.0
        spreads = partial[2] - near * near * (1.0 / 64.0)
        whole = jnp.sum(jnp.sum(totals, axis=0, keepdims=True), axis=1, keepdims=True)
        offset = totals - whole * (1.0 / 2048.0)
        spreads = spreads + offset * offset * (1.0 / 64.0)
        spread = jnp.sum(jnp.sum(spreads, axis=0, keepdims=True), axis=1, keepdims=True)
        packed = pack_stats(whole, spread)
        stat_own[slot] = packed
        stat_a[slot, column] = packed
        each_column(
            lambda r: remote(
                stat_own.at[slot], stat_a.at[slot, column], 0, slot, device(plane, r)
            ).start()
        )

    def relay_stats(slot):
        arrived(stat_a.at[slot, pl.ds(0, COLUMN - 1)], 0, slot)
        total, spread = combine(stat_a[slot, :, 0, :], stat_a[slot, :, 1, :], COLUMN, UNIT_CELLS)
        packed = pack_stats(total, spread)
        stat_mid[slot] = packed
        stat_b[slot, plane] = packed
        each_plane(
            lambda p: remote(
                stat_mid.at[slot], stat_b.at[slot, plane], 1, slot, device(p, column)
            ).start()
        )

    def mixture_stats(slot):
        arrived(stat_b.at[slot, pl.ds(0, PLANE - 1)], 1, slot)
        total, spread = combine(stat_b[slot, :, 0, :], stat_b[slot, :, 1, :], PLANE, COLUMN_CELLS)
        mean = total * (1.0 / MIX_CELLS)
        scale = lax.rsqrt(spread * (1.0 / MIX_CELLS) + EPSILON)
        return (
            jnp.concatenate([mean, mean], axis=1),
            jnp.concatenate([scale, scale], axis=1),
        )

    def carry(b):
        mean, scale = mixture_stats(b)
        for s in range(2):
            normed = (y[b, s] - mean) * scale * ggain_ref[0:1] + gbias_ref[0:1]
            carried[b, s] = (normed + state[b, s].astype(F32)).astype(BF)
        remote(
            carried.at[b, :, other_half, :], pair_in.at[b, core], 2, b, device(plane, partner)
        ).start()
        pair_in[b, core] = carried[b, :, half, :]

    def regroup(b):
        arrived(pair_in.at[b, 0], 2, b)
        for c in range(2):
            lanes = slice(c * 128, (c + 1) * 128)
            for s in range(4):
                flat[c, pl.ds(s, 128, stride=4), :] = pair_in[b, s // 2, s % 2, :, lanes].astype(
                    F32
                )
            chip_out[b, :, :, lanes] = flat[c].reshape(CHIPS, 8, 128).astype(BF)
        chip_in[b, chip] = chip_out[b, chip]
        each_chip(
            lambda x, y_, z: remote(
                chip_out.at[b, x * 16 + y_ * 4 + z], chip_in.at[b, chip],
                3, b, chip_device(x, y_, z, core),
            ).start()
        )

    def regroup_back(b):
        arrived(back_in.at[b, pl.ds(0, CHIPS - 1)], 4, b)
        for c in range(2):
            lanes = slice(c * 128, (c + 1) * 128)
            flat[c] = back_in[b, :, :, lanes].reshape(512, 128).astype(F32)
            for s in range(4):
                pair_out[b, s // 2, s % 2, :, lanes] = flat[c, pl.ds(s, 128, stride=4), :].astype(
                    BF
                )
        remote(
            pair_out.at[b, 1 - core], back.at[b, :, half, :], 5, b, device(plane, partner)
        ).start()
        back[b, :, half, :] = pair_out[b, core]

    def finish(b):
        mean, scale = mixture_stats(4 + b)
        arrived(back.at[b, :, pl.ds(0, 128), :], 5, b)
        for s in range(2):
            normed = (back[b, s].astype(F32) - mean) * scale * ggain_ref[1:2] + gbias_ref[1:2]
            out_ref[b, s] = (normed + carried[b, s].astype(F32)).astype(BF)

    def step(t, _):
        def when(first, work, count=4):
            due = (t >= first) & (t <= first + 2 * count - 2) & (lax.rem(t, 2) == first % 2)
            pl.when(due)(lambda: work(lax.div(t - first, 2)))

        pl.when(t == 1)(lambda: loaded(1))
        pl.when(t == 2)(lambda: loaded(2))

        @pl.when(t == 8)
        def _():
            loaded(3)
            turn(1)

        pl.when(t == 1)(lambda: pl.semaphore_wait(barrier, CHIPS - 1 + 4))
        unit = jnp.where(t < 8, t, t - (V_AT - 8))
        busy = (t < 8) | ((t >= V_AT) & (t < V_AT + 8))
        pl.when(busy & (lax.rem(t, 2) == 0))(lambda: first_half(unit))

        @pl.when(busy & (lax.rem(t, 2) == 1))
        def _():
            second_half(unit)
            start_stats(lax.div(unit, 2))
            pl.when(t >= V_AT)(lambda: send_back(lax.div(unit - 8, 2)))

        when(S2_AT, relay_stats)
        when(V_AT + S2_AT, lambda b: relay_stats(4 + b))
        when(N_AT, carry)
        when(R_AT, regroup)
        when(RR_AT, regroup_back)
        when(F_AT, finish)
        return 0

    loaded(0)
    turn(0)
    lax.fori_loop(0, F_AT + 7, step, 0)

    def drain(b, _):
        for slot in (b, 4 + b):
            left(stat_a.at[slot, pl.ds(0, COLUMN - 1)], 0, slot)
            left(stat_b.at[slot, pl.ds(0, PLANE - 1)], 1, slot)
        left(pair_in.at[b, 0], 2, b)
        left(chip_in.at[b, pl.ds(0, CHIPS - 1)], 3, b)
        left(back_in.at[b, pl.ds(0, CHIPS - 1)], 4, b)
        left(pair_out.at[b, 0], 5, b)
        return 0

    lax.fori_loop(0, MIX, drain, 0)


def on_device(mixture, w_attn, w_up, w_down, norm_gain, norm_bias, group_gain, group_bias):
    hbm = pl.BlockSpec(memory_space=pltpu.HBM)
    return pl.pallas_call(
        kernel,
        name="dual_path",
        out_shape=jax.ShapeDtypeStruct(mixture.shape, BF),
        in_specs=[hbm] * 9,
        out_specs=pl.BlockSpec(memory_space=pltpu.VMEM),
        scratch_shapes=[
            pltpu.VMEM((2, 4, D, D), BF),
            pltpu.VMEM((2, D, 4 * D), BF),
            pltpu.VMEM((2, 4 * D, D), BF),
            pltpu.VMEM((2, 2, D), F32),
            pltpu.VMEM((2, 2, D), F32),
            pltpu.VMEM((2, D), F32),
            pltpu.VMEM((2, D), F32),
            pltpu.VMEM((2, LENGTH, D), F32),
            pltpu.VMEM((MIX, 2, LENGTH, D), BF),
            pltpu.VMEM((2, 2 * D, D), BF),
            pltpu.VMEM((2, LENGTH, D), F32),
            pltpu.VMEM((MIX, 2, LENGTH, D), F32),
            pltpu.VMEM((MIX, 2, LENGTH, D), BF),
            pltpu.VMEM((MIX, 2, 2, 128, D), BF),
            pltpu.VMEM((MIX, CHIPS, 8, D), BF),
            pltpu.VMEM((MIX, CHIPS, 8, D), BF),
            pltpu.VMEM((MIX, CHIPS, 8, D), BF),
            pltpu.VMEM((MIX, CHIPS, 8, D), BF),
            pltpu.VMEM((MIX, 2, 2, 128, D), BF),
            pltpu.VMEM((MIX, 2, LENGTH, D), BF),
            pltpu.VMEM((2, 512, 128), F32),
            pltpu.VMEM((3, 8, D), F32),
            pltpu.VMEM((8, 8, 128), F32),
            pltpu.VMEM((8, COLUMN, 8, 128), F32),
            pltpu.VMEM((8, 8, 128), F32),
            pltpu.VMEM((8, PLANE, 8, 128), F32),
            pltpu.SemaphoreType.DMA((6, 8)),
            pltpu.SemaphoreType.DMA((6, 8)),
            pltpu.SemaphoreType.DMA((4, 5)),
        ],
        compiler_params=pltpu.CompilerParams(
            collective_id=0, has_side_effects=True, vmem_limit_bytes=60 * 1024 * 1024
        ),
    )(
        mixture, w_attn, w_up, w_down, norm_gain, norm_bias, group_gain, group_bias,
        jnp.asarray(position_tables()),
    )


def solution(mesh):
    split = P(None, ("wide", "narrow"), None, None)
    return jax.shard_map(
        on_device, mesh=mesh, in_specs=(split,) + (P(),) * 7, out_specs=split, check_vma=False
    )
```

time: 102 us -> 64.6 us (0.63)
  Pallas kernels: 91.7 us -> 62.2 us
  local copies, waits for them, and re-layouts: 9.65 us -> 2.26 us
    pallas_call x1, Pallas kernels: 91.7 us -> 62.2 us  [on_device(): pl.pallas_call(kernel, name='dual_path', out_shape=jax.ShapeDtypeStruct(m...]
    unnamed x19 -> x1, local copies, waits for them, and re-layouts: 9.65 us -> 2.26 us
where the time goes in v2:
time: 64.6 us; the launch traced here: 64.4 us
  Pallas kernels  62.2 us (96%)
  local copies, waits for them, and re-layouts  2.26 us (3%)
    pallas_call x1, Pallas kernels, on_device(): pl.pallas_call(kernel, name='dual_path', out_shape=jax.ShapeDtypeStruct(m...  62.2 us
    unnamed x1, local copies, waits for them, and re-layouts  2.26 us

profile of v2, /device:TPU:1, one launch (start us, length us, event | category | flops | bytes accessed | tf_op | source)
XLA Modules:
  0.0 64.4 jit_solution(6632503981920645871)
XLA Ops:
  0.0 62.2 %dual_path.1 = bf16[4,2,256,256]{3,2,1,0:T(8,128)(2,1)} custom-call(bf16[4,2,256,256]{3,2,1,0:T(8,128)(2,1)} %mix_ref.1, bf16[2,4,256,256]{3,2,1,0:T(8,128)(2,1)} %attn_hbm.1, bf16[2,256,1024]{2,1,0:T(8,128)(2,1)} %up_hbm.1, bf16[2,1024,256]{2,1,0:T(8,128)(2,1)} %down_hbm.1, f32[2,2,256]{2,1,0:T(2,128)} %gain_hbm.1, f32[2,2,256]{2,1,0:T(2,128)} %bias_hbm.1, ...), custom_call_target="tpu_custom_call" | custom-call | tf_op jit(solution)/shard_map/dual_path/pallas_call | solution.py:391
  62.2 2.3 %copy.11 = bf16[4,2,256,256]{3,2,1,0:T(8,128)(2,1)} copy(bf16[4,2,256,256]{3,2,1,0:T(8,128)(2,1)} %dual_path.1) | data formatting | bytes 2097152

commit v3 on v2

--- a/solution.py
+++ b/solution.py
@@ -28,12 +28,13 @@
 FAR_FIRST = sorted(
     range(1, CHIPS), key=lambda k: -sum((0, 1, 2, 1)[k // d % 4] for d in (1, 4, 16))
 )
-S2_AT = 3
+S2_AT = 4
 V_AT = 14
 N_AT = 7
 R_AT = 8
 RR_AT = 20
 F_AT = 22
+S2V_AT = 18
 
 
 def position_tables():
@@ -176,9 +177,8 @@
     def greet(where):
         pl.semaphore_signal(barrier, inc=1, device_id=where, device_id_type=MESH)
 
-    each_chip(lambda x, y_, z: greet(chip_device(x, y_, z, core)))
-    for z in range(4):
-        greet(device(plane, z * 2 + (1 - core)))
+    each_column(lambda r: greet(device(plane, r)))
+    each_plane(lambda p: greet(device(p, column)))
 
     def turn(l):
         for i, j in ((0, 0), (1, 2)):
@@ -350,7 +350,6 @@
             loaded(3)
             turn(1)
 
-        pl.when(t == 1)(lambda: pl.semaphore_wait(barrier, CHIPS - 1 + 4))
         unit = jnp.where(t < 8, t, t - (V_AT - 8))
         busy = (t < 8) | ((t >= V_AT) & (t < V_AT + 8))
         pl.when(busy & (lax.rem(t, 2) == 0))(lambda: first_half(unit))
@@ -358,11 +357,12 @@
         @pl.when(busy & (lax.rem(t, 2) == 1))
         def _():
             second_half(unit)
+            pl.when(t == 1)(lambda: pl.semaphore_wait(barrier, COLUMN - 1 + PLANE - 1))
             start_stats(lax.div(unit, 2))
             pl.when(t >= V_AT)(lambda: send_back(lax.div(unit - 8, 2)))
 
         when(S2_AT, relay_stats)
-        when(V_AT + S2_AT, lambda b: relay_stats(4 + b))
+        when(S2V_AT, lambda b: relay_stats(4 + b))
         when(N_AT, carry)
         when(R_AT, regroup)
         when(RR_AT, regroup_back)

time: 64.6 us -> 60.3 us (0.933)
  Pallas kernels: 62.2 us -> 57.9 us
    pallas_call x1, Pallas kernels: 62.2 us -> 57.9 us  [on_device(): pl.pallas_call(kernel, name='dual_path', out_shape=jax.ShapeDtypeStruct(m...]
where the time goes in v3:
time: 60.3 us; the launch traced here: 60.1 us
  Pallas kernels  57.9 us (96%)
  local copies, waits for them, and re-layouts  2.26 us (4%)
    pallas_call x1, Pallas kernels, on_device(): pl.pallas_call(kernel, name='dual_path', out_shape=jax.ShapeDtypeStruct(m...  57.9 us
    unnamed x1, local copies, waits for them, and re-layouts  2.26 us

profile of v3, /device:TPU:1, one launch (start us, length us, event | category | flops | bytes accessed | tf_op | source)
XLA Modules:
  0.0 60.1 jit_solution(6102833155678456184)
XLA Ops:
  0.0 57.9 %dual_path.1 = bf16[4,2,256,256]{3,2,1,0:T(8,128)(2,1)} custom-call(bf16[4,2,256,256]{3,2,1,0:T(8,128)(2,1)} %mix_ref.1, bf16[2,4,256,256]{3,2,1,0:T(8,128)(2,1)} %attn_hbm.1, bf16[2,256,1024]{2,1,0:T(8,128)(2,1)} %up_hbm.1, bf16[2,1024,256]{2,1,0:T(8,128)(2,1)} %down_hbm.1, f32[2,2,256]{2,1,0:T(2,128)} %gain_hbm.1, f32[2,2,256]{2,1,0:T(2,128)} %bias_hbm.1, ...), custom_call_target="tpu_custom_call" | custom-call | tf_op jit(solution)/shard_map/dual_path/pallas_call | solution.py:391
  57.9 2.3 %copy.11 = bf16[4,2,256,256]{3,2,1,0:T(8,128)(2,1)} copy(bf16[4,2,256,256]{3,2,1,0:T(8,128)(2,1)} %dual_path.1) | data formatting | bytes 2097152

commit v4 on v3

--- a/solution.py
+++ b/solution.py
@@ -35,6 +35,7 @@
 RR_AT = 20
 F_AT = 22
 S2V_AT = 18
+FIRST_AT = 2
 
 
 def position_tables():
@@ -68,18 +69,15 @@
     values = [part[D:].astype(BF) for part in both]
     keys = [dot(rows, wk).astype(BF) for rows in normed]
     ones = jnp.ones((16, LENGTH), BF)
-    after = []
-    for state, query, key, value in zip(states, queries, keys, values):
-        rows = [slice(h * HEAD, (h + 1) * HEAD) for h in range(HEADS)]
-        scores = [dot(key[:, r], query[r]) for r in rows]
-        weights = [
-            jnp.exp2(part - jnp.max(part, axis=0, keepdims=True)).astype(BF) for part in scores
-        ]
-        summed = [
-            dot(jnp.concatenate([value[r], ones], axis=0), part) for r, part in zip(rows, weights)
-        ]
-        heads = [(part[:HEAD] * (1.0 / part[HEAD : HEAD + 1])).astype(BF) for part in summed]
-        after.append(jnp.concatenate(heads, axis=0).T)
+    rows = [slice(h * HEAD, (h + 1) * HEAD) for h in range(HEADS)]
+    scores = [dot(key[:, r], query[r]) for query, key in zip(queries, keys) for r in rows]
+    weights = [jnp.exp2(part - jnp.max(part, axis=0, keepdims=True)).astype(BF) for part in scores]
+    padded = [jnp.concatenate([value[r], ones], axis=0) for value in values for r in rows]
+    summed = [dot(value, part) for value, part in zip(padded, weights)]
+    heads = [(part[:HEAD] * (1.0 / part[HEAD : HEAD + 1])).astype(BF) for part in summed]
+    after = [
+        jnp.concatenate(heads[i : i + HEADS], axis=0).T for i in range(0, len(heads), HEADS)
+    ]
     return [state + dot(rows, wo) for state, rows in zip(states, after)]
 
 
@@ -198,7 +196,7 @@
             arrived(chip_in.at[b, pl.ds(0, CHIPS - 1)], 3, b)
             for c in range(2):
                 lanes = slice(c * 128, (c + 1) * 128)
-                flat[c] = chip_in[b, :, :, lanes].reshape(512, 128).astype(F32)
+                flat[c, :512] = chip_in[b, :, :, lanes].reshape(512, 128).astype(F32)
                 for f in range(2):
                     for s in range(4):
                         middle[f, s * CHIPS : (s + 1) * CHIPS, lanes] = flat[
@@ -229,9 +227,9 @@
             offset = out.reshape(LENGTH // 8, 8, D) - pivot[None]
             near = near + jnp.sum(offset, axis=0)
             square = square + jnp.sum(offset * offset, axis=0)
-        partial[0] = pivot
-        partial[1] = near
-        partial[2] = square
+        partial[lax.rem(b, 2), 0] = pivot
+        partial[lax.rem(b, 2), 1] = near
+        partial[lax.rem(b, 2), 2] = square
 
     def send_back(b):
         for c in range(2):
@@ -241,7 +239,7 @@
                     flat[c, pl.ds(4 * f + s, CHIPS, stride=8), :] = y[
                         b, f, s * CHIPS : (s + 1) * CHIPS, lanes
                     ]
-            back_out[b, :, :, lanes] = flat[c].reshape(CHIPS, 8, 128).astype(BF)
+            back_out[b, :, :, lanes] = flat[c, :512].reshape(CHIPS, 8, 128).astype(BF)
         back_in[b, chip] = back_out[b, chip]
         each_chip(
             lambda x, y_, z: remote(
@@ -251,9 +249,9 @@
         )
 
     def start_stats(slot):
-        near = partial[1]
-        totals = near + partial[0] * 64.0
-        spreads = partial[2] - near * near * (1.0 / 64.0)
+        start, near, square = (partial[lax.rem(slot, 2), i] for i in range(3))
+        totals = near + start * 64.0
+        spreads = square - near * near * (1.0 / 64.0)
         whole = jnp.sum(jnp.sum(totals, axis=0, keepdims=True), axis=1, keepdims=True)
         offset = totals - whole * (1.0 / 2048.0)
         spreads = spreads + offset * offset * (1.0 / 64.0)
@@ -307,7 +305,7 @@
                 flat[c, pl.ds(s, 128, stride=4), :] = pair_in[b, s // 2, s % 2, :, lanes].astype(
                     F32
                 )
-            chip_out[b, :, :, lanes] = flat[c].reshape(CHIPS, 8, 128).astype(BF)
+            chip_out[b, :, :, lanes] = flat[c, :512].reshape(CHIPS, 8, 128).astype(BF)
         chip_in[b, chip] = chip_out[b, chip]
         each_chip(
             lambda x, y_, z: remote(
@@ -320,7 +318,7 @@
         arrived(back_in.at[b, pl.ds(0, CHIPS - 1)], 4, b)
         for c in range(2):
             lanes = slice(c * 128, (c + 1) * 128)
-            flat[c] = back_in[b, :, :, lanes].reshape(512, 128).astype(F32)
+            flat[c, :512] = back_in[b, :, :, lanes].reshape(512, 128).astype(F32)
             for s in range(4):
                 pair_out[b, s // 2, s % 2, :, lanes] = flat[c, pl.ds(s, 128, stride=4), :].astype(
                     BF
@@ -354,11 +352,15 @@
         busy = (t < 8) | ((t >= V_AT) & (t < V_AT + 8))
         pl.when(busy & (lax.rem(t, 2) == 0))(lambda: first_half(unit))
 
+        @pl.when(t == FIRST_AT)
+        def _():
+            pl.semaphore_wait(barrier, COLUMN - 1 + PLANE - 1)
+            start_stats(0)
+
         @pl.when(busy & (lax.rem(t, 2) == 1))
         def _():
             second_half(unit)
-            pl.when(t == 1)(lambda: pl.semaphore_wait(barrier, COLUMN - 1 + PLANE - 1))
-            start_stats(lax.div(unit, 2))
+            pl.when(t != 1)(lambda: start_stats(lax.div(unit, 2)))
             pl.when(t >= V_AT)(lambda: send_back(lax.div(unit - 8, 2)))
 
         when(S2_AT, relay_stats)
@@ -415,8 +417,8 @@
             pltpu.VMEM((MIX, CHIPS, 8, D), BF),
             pltpu.VMEM((MIX, 2, 2, 128, D), BF),
             pltpu.VMEM((MIX, 2, LENGTH, D), BF),
-            pltpu.VMEM((2, 512, 128), F32),
-            pltpu.VMEM((3, 8, D), F32),
+            pltpu.VMEM((2, 520, 128), F32),
+            pltpu.VMEM((2, 3, 8, D), F32),
             pltpu.VMEM((8, 8, 128), F32),
             pltpu.VMEM((8, COLUMN, 8, 128), F32),
             pltpu.VMEM((8, 8, 128), F32),

time: 60.3 us -> 60.3 us (level)
  no operation moved by 1% of the time
where the time goes in v4:
time: 60.3 us; the launch traced here: 60.2 us
  Pallas kernels  57.9 us (96%)
  local copies, waits for them, and re-layouts  2.26 us (4%)
    pallas_call x1, Pallas kernels, on_device(): pl.pallas_call(kernel, name='dual_path', out_shape=jax.ShapeDtypeStruct(m...  57.9 us
    unnamed x1, local copies, waits for them, and re-layouts  2.26 us

profile of v4, /device:TPU:1, one launch (start us, length us, event | category | flops | bytes accessed | tf_op | source)
XLA Modules:
  0.0 60.2 jit_solution(4563846148162499433)
XLA Ops:
  0.0 57.9 %dual_path.1 = bf16[4,2,256,256]{3,2,1,0:T(8,128)(2,1)} custom-call(bf16[4,2,256,256]{3,2,1,0:T(8,128)(2,1)} %mix_ref.1, bf16[2,4,256,256]{3,2,1,0:T(8,128)(2,1)} %attn_hbm.1, bf16[2,256,1024]{2,1,0:T(8,128)(2,1)} %up_hbm.1, bf16[2,1024,256]{2,1,0:T(8,128)(2,1)} %down_hbm.1, f32[2,2,256]{2,1,0:T(2,128)} %gain_hbm.1, f32[2,2,256]{2,1,0:T(2,128)} %bias_hbm.1, ...), custom_call_target="tpu_custom_call" | custom-call | tf_op jit(solution)/shard_map/dual_path/pallas_call | solution.py:393
  57.9 2.3 %copy.11 = bf16[4,2,256,256]{3,2,1,0:T(8,128)(2,1)} copy(bf16[4,2,256,256]{3,2,1,0:T(8,128)(2,1)} %dual_path.1) | data formatting | bytes 2097152

commit v5 on v4

--- a/solution.py
+++ b/solution.py
@@ -364,7 +364,8 @@
             pl.when(t >= V_AT)(lambda: send_back(lax.div(unit - 8, 2)))
 
         when(S2_AT, relay_stats)
-        when(S2V_AT, lambda b: relay_stats(4 + b))
+        when(S2V_AT, lambda b: relay_stats(4 + b), 3)
+        pl.when(t == 23)(lambda: relay_stats(7))
         when(N_AT, carry)
         when(R_AT, regroup)
         when(RR_AT, regroup_back)

time: 60.3 us -> 60.2 us (level)
  no operation moved by 1% of the time
where the time goes in v5:
time: 60.2 us; the launch traced here: 60.1 us
  Pallas kernels  57.8 us (96%)
  local copies, waits for them, and re-layouts  2.26 us (4%)
    pallas_call x1, Pallas kernels, on_device(): pl.pallas_call(kernel, name='dual_path', out_shape=jax.ShapeDtypeStruct(m...  57.8 us
    unnamed x1, local copies, waits for them, and re-layouts  2.26 us

profile of v5, /device:TPU:1, one launch (start us, length us, event | category | flops | bytes accessed | tf_op | source)
XLA Modules:
  0.0 60.1 jit_solution(14727128865734291578)
XLA Ops:
  0.0 57.8 %dual_path.1 = bf16[4,2,256,256]{3,2,1,0:T(8,128)(2,1)} custom-call(bf16[4,2,256,256]{3,2,1,0:T(8,128)(2,1)} %mix_ref.1, bf16[2,4,256,256]{3,2,1,0:T(8,128)(2,1)} %attn_hbm.1, bf16[2,256,1024]{2,1,0:T(8,128)(2,1)} %up_hbm.1, bf16[2,1024,256]{2,1,0:T(8,128)(2,1)} %down_hbm.1, f32[2,2,256]{2,1,0:T(2,128)} %gain_hbm.1, f32[2,2,256]{2,1,0:T(2,128)} %bias_hbm.1, ...), custom_call_target="tpu_custom_call" | custom-call | tf_op jit(solution)/shard_map/dual_path/pallas_call | solution.py:394
  57.8 2.3 %copy.11 = bf16[4,2,256,256]{3,2,1,0:T(8,128)(2,1)} copy(bf16[4,2,256,256]{3,2,1,0:T(8,128)(2,1)} %dual_path.1) | data formatting | bytes 2097152
